TPU v7x, 256 devices: a whole 4x4x8 slice. The times are simulated.
256 devices in a mesh: group: 8 (over z), shard: 32 (over x, y, core).
Axes of the slice: x: 4, y: 4, z: 8, core: 2. Of those that a mesh axis runs over, the one named last changes fastest.
Arguments:
- queries: bfloat16 [1536, 1024], P(('group', 'shard')), may hold values from -12 to 12
- candidates: bfloat16 [1048576, 1024], P(('group', 'shard')), may hold values from -4 to 4
- targets: int32 [1536], replicated, may hold values from 0 to 1048575
Outputs:
- losses: float32 [1536], replicated
- mean_loss: float32 [], replicated
All inputs are finite; a program needn't handle non-finite values.
Results may differ from a plain program's by a relative error of at most 0.0003.
Values may be sent and summed in bfloat16 or wider, within the bound.
A program may use at most 64 MiB of HBM per device.

v0:
```python
import math
import jax
import jax.numpy as jnp
from jax import lax
from jax.sharding import Mesh
from jax.sharding import PartitionSpec as P

SHARD = ("shard_0", "shard_1", "shard_2")
GROUP_SHARD = ("group", "shard_0", "shard_1", "shard_2")


def laid_out(tiles, dim):
    shape = list(tiles.shape[1:])
    shape[dim] *= tiles.shape[0]
    return jnp.moveaxis(tiles, 0, dim).reshape(shape)


def gather_in_order(value, axes, order):
    tiles = value[None]
    for k in order:
        tiles = lax.all_gather(tiles, axes[k], axis=0, tiled=True)
    held = [lax.axis_size(axes[k]) for k in reversed(order)]
    tiles = tiles.reshape(*held, *value.shape)
    turned = sorted(range(len(order)), key=lambda place: order[len(order) - 1 - place])
    return tiles.transpose(*turned, *range(len(order), tiles.ndim)).reshape(-1, *value.shape)


def gather_axes(value, axes, order, dim):
    return laid_out(gather_in_order(value, axes, order), dim)


def from_everyone(value, axis):
    copies = jnp.broadcast_to(value, (lax.axis_size(axis), *value.shape))
    return lax.all_to_all(copies, axis, split_axis=0, concat_axis=0, tiled=True)


def collected_together(value, axis):
    leaves = jax.tree.leaves(value)
    order = sorted(range(len(leaves)), key=lambda k: -leaves[k].size)
    width = (1, *leaves[order[0]].shape)[-1]
    lines = [
        jnp.pad(leaves[k].reshape(-1), (0, -leaves[k].size % width)).reshape(-1, width)
        for k in order
    ]
    both, at, found = (from_everyone(jnp.concatenate(lines), axis), 0, {})
    for k, line in zip(order, lines):
        share = both[:, at : at + len(line)].reshape(len(both), -1)
        found[k] = share[:, : leaves[k].size].reshape(-1, *leaves[k].shape)
        at += len(line)
    numbers = iter(range(len(leaves)))
    return jax.tree.map(lambda _: found[next(numbers)], value)


def folded_in_pairs(pieces, combine):
    while len(jax.tree.leaves(pieces)[0]) > 1:
        pieces = jax.vmap(combine)(
            *(jax.tree.map(lambda part: part[side::2], pieces) for side in (0, 1))
        )
    return jax.tree.map(lambda part: part[0], pieces)


def combined_all(value, axis, combine):
    pieces = collected_together(value, axis)
    return folded_in_pairs(pieces, combine)


def once_a_type(value, axis):
    leaves, found = (jax.tree.leaves(value), {})
    for leading, a in enumerate(leaves):
        if leading not in found:
            alike = [k for k, b in enumerate(leaves) if b.dtype == a.dtype]
            got = (
                collected_together([leaves[k] for k in alike], axis)
                if len(alike) > 1
                else [from_everyone(a, axis)]
            )
            for k, b in zip(alike, got):
                found[k] = b
    numbers = iter(range(len(leaves)))
    return jax.tree.map(lambda _: found[next(numbers)], value)


def merged(value, axis, combine):
    pieces = once_a_type(value, axis)
    return folded_in_pairs(pieces, combine)


def combine(first, second):
    top = jnp.maximum(first[0], second[0])
    total = first[1] * jnp.exp(first[0] - top) + second[1] * jnp.exp(second[0] - top)
    return (top, total, first[2] + second[2])


def score_rows(piece, candidates, chosen_targets, owner):
    rows = candidates.shape[0]
    local = chosen_targets - owner * rows
    owned = (local >= 0) & (local < rows)
    chosen = jnp.take(candidates, jnp.clip(local, 0, rows - 1), axis=0)
    products = jnp.sum(piece.astype(jnp.float32) * chosen.astype(jnp.float32), axis=1)
    picked = jnp.where(owned, products, jnp.float32(0.0))
    count = piece.shape[0]
    block = math.gcd(count, 512)
    panels = piece.reshape(count // block, block, piece.shape[1])

    def score_panel(panel):
        scores = jnp.dot(panel, candidates.T, preferred_element_type=jnp.float32)
        peak = jnp.max(scores, axis=1)
        return (peak, jnp.sum(jnp.exp(scores - peak[:, None]), axis=1))

    peaks, sums = lax.map(score_panel, panels)
    return (peaks.reshape(count), sums.reshape(count), picked)


def on_device(queries, candidates, targets):
    owner = lax.axis_index("group") * lax.axis_size(SHARD) + lax.axis_index(SHARD)
    every = gather_axes(queries, GROUP_SHARD, (1, 0, 2, 3), 0)
    top, total, picked = score_rows(every, candidates, targets, owner)
    inner = combined_all((top, total, picked), SHARD, combine)
    top, total, picked = merged(inner, "group", combine)
    losses = top + jnp.log(total) - picked
    return (losses, jnp.mean(losses))


def solution(mesh):
    finer = Mesh(
        mesh.devices.reshape(mesh.shape["group"], 4, 4, 2),
        ("group", "shard_0", "shard_1", "shard_2"),
    )
    in_specs = (P(GROUP_SHARD, None), P(GROUP_SHARD, None), P())
    out_specs = (P(), P())
    return jax.shard_map(
        on_device, mesh=finer, in_specs=in_specs, out_specs=out_specs, check_vma=False
    )
```

profile of v0, /device:TPU:1, one launch (start us, length us, event | category | flops | bytes accessed | tf_op | source)
XLA Modules:
  0.0 195.4 jit_solution(15849809175005774843)
XLA Ops:
  7.2 0.0 all-gather.5.cloned.1.call-start
  7.2 10.4 %all-gather.1 = bf16[4,6,1024]{2,1,0:T(8,128)(2,1)S(1)} all-gather(bf16[1,6,1024]{2,1,0:T(8,128)(2,1)} %bitcast.56), channel_id=2, replica_groups=mesh['group'=8,'shard_0'=4,'shard_1'=4,'shard_2'=2] {'shard_0'}, dimensions={0}, use_global_device_ids=true | all-gather | bytes 61440 | tf_op jit(solution)/shard_map/all_gather | solution.py:21
  17.6 23.3 %all_gather.13 = bf16[32,6,1024]{2,1,0:T(8,128)(2,1)S(1)} all-gather(bf16[4,6,1024]{2,1,0:T(8,128)(2,1)S(1)} %all-gather.1), channel_id=1, replica_groups=mesh['group'=8,'shard_0'=4,'shard_1'=4,'shard_2'=2] {'group'}, dimensions={0}, use_global_device_ids=true | all-gather | bytes 442368 | tf_op jit(solution)/shard_map/all_gather | solution.py:21
  40.9 1.0 copy.36
  41.8 0.0 all-gather.5.cloned.1.call-update
  41.9 0.0 all-gather.7.cloned.1.call-start
  41.9 36.5 %all-gather.5.cloned.1.call-done = bf16[128,6,1024]{2,0,1:T(8,128)(2,1)} async-done(((bf16[32,6,1024]{2,0,1:T(8,128)(2,1)}), bf16[128,6,1024]{2,0,1:T(8,128)(2,1)}) %all-gather.5.cloned.1.call-update) | async-done | bytes 1572880 | tf_op jit(solution)/shard_map/all_gather | solution.py:21
  78.4 0.0 all-gather.7.cloned.1.call-update
  78.5 0.7 compare_and_fusion
  79.2 11.6 %gather_fusion = bf16[1536,1024]{1,0:T(8,128)(2,1)S(1)} fusion(bf16[4096,1024]{1,0:T(8,128)(2,1)} %param.6, s32[2048]{0:T(1024)S(1)} %pad_clamp_fusion), kind=kCustom, calls=%fused_computation | custom fusion | bytes 6297600 | tf_op jit(solution)/shard_map/jit(_take)/gather | solution.py:98
  90.8 2.9 %gather.7 = bf16[8,4,4,2,6,1024]{5,4,3,2,1,0:T(8,128)(2,1)} reshape(bf16[1536,1024]{1,0:T(8,128)(2,1)S(1)} %gather_fusion) | data formatting | bytes 6291456 | tf_op jit(solution)/shard_map/jit(_take)/gather | solution.py:98
  93.7 0.2 broadcast_in_dim.36
  93.9 0.6 copy.38
  94.5 4.1 %all-gather.7.cloned.1.call-done = bf16[256,6,1024]{2,0,1:T(8,128)(2,1)} async-done(((bf16[128,6,1024]{2,0,1:T(8,128)(2,1)}), bf16[256,6,1024]{2,0,1:T(8,128)(2,1)}) %all-gather.7.cloned.1.call-update) | async-done | bytes 3145744 | tf_op jit(solution)/shard_map/all_gather | solution.py:21
  98.6 4.0 %reshape.57 = bf16[2,4,8,4,6,1024]{5,3,2,1,0,4:T(4,128)(2,1)S(1)} reshape(bf16[256,6,1024]{2,0,1:T(8,128)(2,1)} %all-gather.7.cloned.1.call-done) | data formatting | bytes 6291456 | tf_op jit(solution)/shard_map/reshape | solution.py:23
  102.6 0.0 copy-start
  102.6 7.8 %multiply_reduce_fusion = f32[8,4,4,2,6]{1,0,2,3,4:T(8,128)S(1)} fusion(bf16[8,4,4,2,6,1024]{5,4,3,2,1,0:T(8,128)(2,1)} %gather.7, pred[8,4,4,2,6]{1,0,2,3,4:T(8,128)(4,1)S(1)} %copy.38, bf16[2,4,8,4,6,1024]{5,3,2,1,0,4:T(4,128)(2,1)S(1)} %reshape.57), kind=kLoop, calls=%fused_computation.6 | loop fusion | flops 7862784 | bytes 6299136 | tf_op jit(solution)/shard_map/reduce_sum | solution.py:99
  110.4 0.5 copy.40
  111.0 0.2 reduce_sum.30
  111.2 0.0 copy-done
  111.2 3.7 %copy.37 = bf16[8,4,4,2,6,1024]{5,4,3,2,1,0:T(8,128)(2,1)} copy(bf16[8,4,4,2,6,1024]{5,1,0,2,3,4:T(4,128)(2,1)S(1)} %bitcast.43) | data formatting | bytes 6291456 | tf_op jit(solution)/shard_map/transpose | solution.py:25
  115.0 4.9 %reshape_reshape_reshape.3 = bf16[3,512,1024]{2,1,0:T(8,128)(2,1)S(1)} reshape(bf16[8,4,4,2,6,1024]{5,4,3,2,1,0:T(8,128)(2,1)} %copy.37) | data formatting | bytes 6291456 | tf_op jit(solution)/shard_map/reshape;reshape;reshape | solution.py:103
  119.8 25.6 %while.12 = (s32[]{:T(128)}, f32[3,512]{1,0:T(4,128)S(1)}, f32[3,512]{1,0:T(4,128)S(1)}, bf16[3,512,1024]{2,1,0:T(8,128)(2,1)S(1)}, bf16[4096,1024]{1,0:T(8,128)(2,1)}, /*index=5*/s32[]{:T(128)}, s32[]{:T(128)}) while((s32[]{:T(128)}, f32[3,512]{1,0:T(4,128)S(1)}, f32[3,512]{1,0:T(4,128)S(1)}, bf16[3,512,1024]{2,1,0:T(8,128)(2,1)S(1)}, ...), condition=%wide.region_3.4_spmd, body=%wide.region_0.0_spmd.sunk | while | flops 4301257728 | bytes 26228824 | solution.py:110
  119.9 7.1 %fusion.16 = (f32[512]{0:T(512)S(1)}, f32[512,4096]{1,0:T(8,128)S(1)}) fusion(bf16[4096,1024]{1,0:T(8,128)(2,1)} %get-tuple-element.123, bf16[3,512,1024]{2,1,0:T(8,128)(2,1)S(1)} %get-tuple-element.122, s32[]{:T(128)} %get-tuple-element.112), kind=kOutput, calls=%fused_computation.39.clone.1 | convolution fusion | flops 4297063936 | bytes 17827844 | tf_op jit(solution)/shard_map/while/body/eval_jaxpr/dot_general | solution.py:106
  127.0 1.3 exponential_reduce_fusion.2
  128.3 0.1 dynamic_update_slice.9
  128.4 7.1 %fusion.16 = (f32[512]{0:T(512)S(1)}, f32[512,4096]{1,0:T(8,128)S(1)}) fusion(bf16[4096,1024]{1,0:T(8,128)(2,1)} %get-tuple-element.123, bf16[3,512,1024]{2,1,0:T(8,128)(2,1)S(1)} %get-tuple-element.122, s32[]{:T(128)} %get-tuple-element.112), kind=kOutput, calls=%fused_computation.39.clone.1 | convolution fusion | flops 4297063936 | bytes 17827844 | tf_op jit(solution)/shard_map/while/body/eval_jaxpr/dot_general | solution.py:106
  135.5 1.3 exponential_reduce_fusion.2
  136.8 0.1 dynamic_update_slice.9
  136.9 7.1 %fusion.16 = (f32[512]{0:T(512)S(1)}, f32[512,4096]{1,0:T(8,128)S(1)}) fusion(bf16[4096,1024]{1,0:T(8,128)(2,1)} %get-tuple-element.123, bf16[3,512,1024]{2,1,0:T(8,128)(2,1)S(1)} %get-tuple-element.122, s32[]{:T(128)} %get-tuple-element.112), kind=kOutput, calls=%fused_computation.39.clone.1 | convolution fusion | flops 4297063936 | bytes 17827844 | tf_op jit(solution)/shard_map/while/body/eval_jaxpr/dot_general | solution.py:106
  144.0 1.3 exponential_reduce_fusion.2
  145.4 0.1 dynamic_update_slice.9
  145.5 0.1 broadcast_in_dim.41
  145.6 20.8 %all_to_all.10 = f32[32,3,1536]{2,1,0:T(4,128)S(1)} all-to-all(f32[32,3,1536]{2,1,0:T(4,128)S(1)} %broadcast_in_dim.41), channel_id=1, replica_groups=mesh['group'=8,'shard_0'=4,'shard_1'=4,'shard_2'=2] {'shard_0','shard_1'..., dimensions={0} | all-to-all | bytes 1179648 | tf_op jit(solution)/shard_map/all_to_all | solution.py:34
  166.5 0.4 fusion.10
  168.0 17.4 %all_to_all.11 = f32[8,3,1536]{2,1,0:T(4,128)S(1)} all-to-all(f32[8,3,1536]{2,1,0:T(4,128)S(1)} %broadcast_in_dim.42), channel_id=1, replica_groups=mesh['group'=8,'shard_0'=4,'shard_1'=4,'shard_2'=2] {'group'}, dimensions={0} | all-to-all | bytes 294912 | tf_op jit(solution)/shard_map/all_to_all | solution.py:34
  185.5 0.1 fusion.11
  186.0 0.7 fusion.8
  (68 shorter events, 1.6 us)
Async XLA Ops:
  7.2 71.3 %all-gather.5.cloned.1.call-start = ((), (), s32[]{:S(2)}) async-start(), calls=%async_computation.2 | async-start | bytes 1966080 | tf_op jit(solution)/shard_map/all_gather | solution.py:21
  41.9 56.7 %all-gather.7.cloned.1.call-start = ((), (), s32[]{:S(2)}) async-start(), calls=%async_computation.3 | async-start | bytes 4718592 | tf_op jit(solution)/shard_map/all_gather | solution.py:21
  102.6 8.6 %copy-start = (s32[1536]{0:T(1024)S(1)}, s32[1536]{0:T(1024)}, u32[]{:S(2)}) copy-start(s32[1536]{0:T(1024)} %param.7) | copy-start | bytes 18436
Sparse Core Ops, SparseCore 0:
  42.0 36.4 all-gather.4
  80.2 18.3 all-gather.6
where the time goes:
time: 196 us; the launch traced here: 195 us
  blocking collectives  71.9 us (37%)
  waiting for transfers between devices  40.6 us (21%)
  local copies, waits for them, and re-layouts  31.7 us (16%)
  matrix products  21.4 us (11%)
  between operations  16.2 us (8%)
  other arithmetic  13.4 us (7%)
    all_gather x2, waiting for transfers between devices, gather_in_order(): tiles = lax.all_gather(tiles, axes[k], axis=0, tiled=True)  40.6 us
    all_to_all x2, blocking collectives, from_everyone(): return lax.all_to_all(copies, axis, split_axis=0, concat_axis=0, tiled=True)  38.3 us
    all_gather x2, blocking collectives, gather_in_order(): tiles = lax.all_gather(tiles, axes[k], axis=0, tiled=True)  33.7 us
    dot_general x3, matrix products, score_panel(): scores = jnp.dot(panel, candidates.T, preferred_element_type=jnp.float32)  21.4 us
    gather x2, local copies, waits for them, and re-layouts, score_rows(): chosen = jnp.take(candidates, jnp.clip(local, 0, rows - 1), axis=0)  14.5 us
    reduce_sum x1, other arithmetic, score_rows(): jnp.sum(piece.astype(jnp.float32) * chosen.astype(jnp.float32), axis=1)  7.8 us
    another operation x1, local copies, waits for them, and re-layouts, score_rows(): panels = piece.reshape(count // block, block, piece.shape[1])  4.87 us
    reshape x1, local copies, waits for them, and re-layouts, gather_in_order(): tiles = tiles.reshape(*held, *value.shape)  4.01 us
  transfers between devices with their start and end apart: 2, of which 2 were waited for; matrix products, arithmetic and copies ran while one was open for 8% of the time, Pallas kernels for 0%

commit v1 on v0

--- a/solution.py
+++ b/solution.py
@@ -18,7 +18,10 @@
 def gather_in_order(value, axes, order):
     tiles = value[None]
     for k in order:
-        tiles = lax.all_gather(tiles, axes[k], axis=0, tiled=True)
+        size = lax.axis_size(axes[k])
+        blocks = jnp.stack([tiles for _ in range(size)])
+        blocks = lax.all_to_all(blocks, axes[k], split_axis=0, concat_axis=0)
+        tiles = jnp.concatenate(blocks, axis=0)
     held = [lax.axis_size(axes[k]) for k in reversed(order)]
     tiles = tiles.reshape(*held, *value.shape)
     turned = sorted(range(len(order)), key=lambda place: order[len(order) - 1 - place])

time: 196 us -> 149 us (0.76)
  waiting for transfers between devices: 40.6 us -> 0.79 us
  between operations: 16.2 us -> 2.85 us
  starting transfers between devices: 0.08 us -> 4.35 us
  local copies, waits for them, and re-layouts: 31.7 us -> 34.2 us
    all_gather x2 -> x0, waiting for transfers between devices: 40.6 us -> none  [gather_in_order(): tiles = lax.all_gather(tiles, axes[k], axis=0, tiled=True)]
    all_to_all x0 -> x3, blocking collectives: none -> 40 us  [gather_in_order(): blocks = lax.all_to_all(blocks, axes[k], split_axis=0, concat_axis=0)]
    all_gather x2 -> x0, blocking collectives: 33.7 us -> none  [gather_in_order(): tiles = lax.all_gather(tiles, axes[k], axis=0, tiled=True)]
    all_to_all x2, blocking collectives: 38.3 us -> 32.5 us  [from_everyone(): return lax.all_to_all(copies, axis, split_axis=0, concat_axis=0, tiled=True)]
    all_to_all x0 -> x3, local copies, waits for them, and re-layouts: none -> 4.97 us  [gather_in_order(): blocks = lax.all_to_all(blocks, axes[k], split_axis=0, concat_axis=0)]
    all_to_all x0 -> x1, starting transfers between devices: none -> 4.35 us  [gather_in_order(): blocks = lax.all_to_all(blocks, axes[k], split_axis=0, concat_axis=0)]
    reshape x1 -> x0, local copies, waits for them, and re-layouts: 4.01 us -> none  [gather_in_order(): tiles = tiles.reshape(*held, *value.shape)]
    another operation x0 -> x5, local copies, waits for them, and re-layouts: none -> 2.37 us  [gather_in_order(): blocks = jnp.stack([tiles for _ in range(size)])]
  transfers between devices with their start and end apart: 2 -> 1, of which waited for: 2 -> 1; matrix products, arithmetic and copies ran while one was open for 8% -> 10% of each run, Pallas kernels for 0% -> 0%
where the time goes in v1:
time: 149 us
  blocking collectives  72.5 us (49%)
  local copies, waits for them, and re-layouts  34.2 us (23%)
  matrix products  21.4 us (14%)
  other arithmetic  12.7 us (9%)
  starting transfers between devices  4.35 us (3%)
  between operations  2.85 us (2%)
    all_to_all x3, blocking collectives, gather_in_order(): blocks = lax.all_to_all(blocks, axes[k], split_axis=0, concat_axis=0)  40 us
    all_to_all x2, blocking collectives, from_everyone(): return lax.all_to_all(copies, axis, split_axis=0, concat_axis=0, tiled=True)  32.5 us
    dot_general x3, matrix products, score_panel(): scores = jnp.dot(panel, candidates.T, preferred_element_type=jnp.float32)  21.4 us
    gather x2, local copies, waits for them, and re-layouts, score_rows(): chosen = jnp.take(candidates, jnp.clip(local, 0, rows - 1), axis=0)  14.4 us
    reduce_sum x1, other arithmetic, score_rows(): jnp.sum(piece.astype(jnp.float32) * chosen.astype(jnp.float32), axis=1)  7.52 us
    all_to_all x3, local copies, waits for them, and re-layouts, gather_in_order(): blocks = lax.all_to_all(blocks, axes[k], split_axis=0, concat_axis=0)  4.97 us
    another operation x1, local copies, waits for them, and re-layouts, score_rows(): panels = piece.reshape(count // block, block, piece.shape[1])  4.88 us
    all_to_all x1, starting transfers between devices, gather_in_order(): blocks = lax.all_to_all(blocks, axes[k], split_axis=0, concat_axis=0)  4.35 us
  transfers between devices with their start and end apart: 1, of which 1 were waited for; matrix products, arithmetic and copies ran while one was open for 10% of the time, Pallas kernels for 0%

profile of v1, /device:TPU:1, one launch (start us, length us, event | category | flops | bytes accessed | tf_op | source)
XLA Modules:
  0.0 148.8 jit_solution(5390928843071028787)
XLA Ops:
  0.6 0.7 stack.12
  1.4 9.1 %all_to_all.30 = bf16[4,1,6,1024]{3,2,1,0:T(8,128)(2,1)S(1)} all-to-all(bf16[4,1,6,1024]{3,2,1,0:T(8,128)(2,1)S(1)} %stack.12), channel_id=1, replica_groups=mesh['group'=8,'shard_0'=4,'shard_1'=4,'shard_2'=2] {'shard_0'}, dimensions={0} | all-to-all | bytes 98304 | tf_op jit(solution)/shard_map/all_to_all | solution.py:23
  10.5 0.1 stack.13
  10.6 19.6 %all_to_all.31 = bf16[8,4,6,1024]{3,1,2,0:T(4,128)(2,1)S(1)} all-to-all(bf16[8,4,6,1024]{3,1,2,0:T(4,128)(2,1)S(1)} %stack.13), channel_id=1, replica_groups=mesh['group'=8,'shard_0'=4,'shard_1'=4,'shard_2'=2] {'group'}, dimensions={0} | all-to-all | bytes 786432 | tf_op jit(solution)/shard_map/all_to_all | solution.py:23
  30.2 0.1 copy.56
  30.4 0.0 copy-start.1
  30.4 0.1 stack_reshape.7
  30.5 1.4 stack.14
  31.8 4.3 %all-to-all-start.2 = ((bf16[4,32,6,1024]{3,1,2,0:T(8,128)(2,1)}), bf16[4,32,6,1024]{3,1,2,0:T(8,128)(2,1)}, u32[]{:S(2)}, u32[]{:S(2)}) async-start(bf16[4,32,6,1024]{3,1,2,0:T(8,128)(2,1)} %stack.14), calls=%async_computation.2 | async-start | bytes 3145728 | tf_op jit(solution)/shard_map/all_to_all | solution.py:23
  36.2 0.0 copy-done.1
  36.3 11.6 %gather_fusion = bf16[1536,1024]{1,0:T(8,128)(2,1)S(1)} fusion(bf16[4096,1024]{1,0:T(8,128)(2,1)} %param.6, s32[2048]{0:T(1024)S(1)} %pad_clamp_fusion), kind=kCustom, calls=%fused_computation | custom fusion | bytes 6297600 | tf_op jit(solution)/shard_map/jit(_take)/gather | solution.py:101
  47.8 2.9 %gather.7 = bf16[8,4,4,2,6,1024]{5,4,3,2,1,0:T(8,128)(2,1)} reshape(bf16[1536,1024]{1,0:T(8,128)(2,1)S(1)} %gather_fusion) | data formatting | bytes 6291456 | tf_op jit(solution)/shard_map/jit(_take)/gather | solution.py:101
  50.7 0.2 broadcast_in_dim.32
  50.9 0.9 copy.60
  51.8 0.8 all-to-all-done.2
  52.6 1.6 %copy.57 = bf16[4,32,6,1024]{3,1,0,2:T(8,128)(2,1)S(1)} copy(bf16[4,32,6,1024]{3,1,2,0:T(8,128)(2,1)} %all-to-all-done.2) | data formatting | bytes 3145728 | tf_op jit(solution)/shard_map/all_to_all | solution.py:23
  54.2 0.3 pad_maximum_fusion
  54.5 11.3 %all_to_all.32 = bf16[2,128,6,1024]{3,1,2,0:T(8,128)(2,1)S(1)} all-to-all(bf16[2,128,6,1024]{3,1,2,0:T(8,128)(2,1)S(1)} %pad_maximum_fusion), channel_id=1, replica_groups=mesh['group'=8,'shard_0'=4,'shard_1'=4,'shard_2'=2] {'shard_2'}, dimensions={0} | all-to-all | bytes 6291456 | tf_op jit(solution)/shard_map/all_to_all | solution.py:23
  65.8 3.2 %copy.58 = bf16[2,128,6,1024]{3,0,2,1:T(2,128)(2,1)S(1)} copy(bf16[2,128,6,1024]{3,1,2,0:T(8,128)(2,1)S(1)} %all_to_all.32) | data formatting | bytes 6291456 | tf_op jit(solution)/shard_map/all_to_all | solution.py:23
  69.0 0.0 copy-start
  69.0 3.3 %copy.59 = bf16[8,4,4,2,6,1024]{5,4,3,2,1,0:T(8,128)(2,1)} copy(bf16[8,4,4,2,6,1024]{5,3,4,1,0,2:T(2,128)(2,1)S(1)} %bitcast.45) | data formatting | bytes 6291456 | tf_op jit(solution)/shard_map/transpose | solution.py:28
  72.3 0.0 copy-done
  72.3 7.5 %multiply_reduce_fusion = f32[8,4,4,2,6]{3,4,1,0,2:T(8,128)S(1)} fusion(bf16[8,4,4,2,6,1024]{5,3,4,1,0,2:T(2,128)(2,1)S(1)} %bitcast.46, pred[8,4,4,2,6]{3,4,1,0,2:T(8,128)(4,1)S(1)} %copy.60, bf16[8,4,4,2,6,1024]{5,4,3,2,1,0:T(8,128)(2,1)S(1)} %copy-done), kind=kLoop, calls=%fused_computation.6 | loop fusion | flops 7862784 | bytes 6299136 | tf_op jit(solution)/shard_map/reduce_sum | solution.py:102
  79.9 0.9 copy.62
  80.7 0.2 reduce_sum.30
  81.0 4.9 %reshape_reshape_reshape.3 = bf16[3,512,1024]{2,1,0:T(8,128)(2,1)S(1)} reshape(bf16[8,4,4,2,6,1024]{5,4,3,2,1,0:T(8,128)(2,1)} %copy.59) | data formatting | bytes 6291456 | tf_op jit(solution)/shard_map/reshape;reshape;reshape | solution.py:106
  85.9 25.6 %while.12 = (s32[]{:T(128)}, f32[3,512]{1,0:T(4,128)S(1)}, f32[3,512]{1,0:T(4,128)S(1)}, bf16[3,512,1024]{2,1,0:T(8,128)(2,1)S(1)}, bf16[4096,1024]{1,0:T(8,128)(2,1)}, /*index=5*/s32[]{:T(128)}, s32[]{:T(128)}) while((s32[]{:T(128)}, f32[3,512]{1,0:T(4,128)S(1)}, f32[3,512]{1,0:T(4,128)S(1)}, bf16[3,512,1024]{2,1,0:T(8,128)(2,1)S(1)}, ...), condition=%wide.region_3.4_spmd, body=%wide.region_0.0_spmd.sunk | while | flops 4301257728 | bytes 26228824 | solution.py:113
  85.9 7.1 %fusion.16 = (f32[512]{0:T(512)S(1)}, f32[512,4096]{1,0:T(8,128)S(1)}) fusion(bf16[4096,1024]{1,0:T(8,128)(2,1)} %get-tuple-element.123, bf16[3,512,1024]{2,1,0:T(8,128)(2,1)S(1)} %get-tuple-element.122, s32[]{:T(128)} %get-tuple-element.112), kind=kOutput, calls=%fused_computation.40.clone.1 | convolution fusion | flops 4297063936 | bytes 17827844 | tf_op jit(solution)/shard_map/while/body/eval_jaxpr/dot_general | solution.py:109
  93.0 1.3 exponential_reduce_fusion.2
  94.3 0.1 dynamic_update_slice.9
  94.4 7.1 %fusion.16 = (f32[512]{0:T(512)S(1)}, f32[512,4096]{1,0:T(8,128)S(1)}) fusion(bf16[4096,1024]{1,0:T(8,128)(2,1)} %get-tuple-element.123, bf16[3,512,1024]{2,1,0:T(8,128)(2,1)S(1)} %get-tuple-element.122, s32[]{:T(128)} %get-tuple-element.112), kind=kOutput, calls=%fused_computation.40.clone.1 | convolution fusion | flops 4297063936 | bytes 17827844 | tf_op jit(solution)/shard_map/while/body/eval_jaxpr/dot_general | solution.py:109
  101.5 1.3 exponential_reduce_fusion.2
  102.9 0.1 dynamic_update_slice.9
  102.9 7.1 %fusion.16 = (f32[512]{0:T(512)S(1)}, f32[512,4096]{1,0:T(8,128)S(1)}) fusion(bf16[4096,1024]{1,0:T(8,128)(2,1)} %get-tuple-element.123, bf16[3,512,1024]{2,1,0:T(8,128)(2,1)S(1)} %get-tuple-element.122, s32[]{:T(128)} %get-tuple-element.112), kind=kOutput, calls=%fused_computation.40.clone.1 | convolution fusion | flops 4297063936 | bytes 17827844 | tf_op jit(solution)/shard_map/while/body/eval_jaxpr/dot_general | solution.py:109
  110.1 1.3 exponential_reduce_fusion.2
  111.4 0.1 dynamic_update_slice.9
  111.5 0.1 broadcast_in_dim.37
  111.6 18.0 %all_to_all.33 = f32[32,3,1536]{2,1,0:T(4,128)S(1)} all-to-all(f32[32,3,1536]{2,1,0:T(4,128)S(1)} %broadcast_in_dim.37), channel_id=1, replica_groups=mesh['group'=8,'shard_0'=4,'shard_1'=4,'shard_2'=2] {'shard_0','shard_1'..., dimensions={0} | all-to-all | bytes 1179648 | tf_op jit(solution)/shard_map/all_to_all | solution.py:37
  129.6 0.4 fusion.10
  131.2 14.5 %all_to_all.34 = f32[8,3,1536]{2,1,0:T(4,128)S(1)} all-to-all(f32[8,3,1536]{2,1,0:T(4,128)S(1)} %broadcast_in_dim.38), channel_id=1, replica_groups=mesh['group'=8,'shard_0'=4,'shard_1'=4,'shard_2'=2] {'group'}, dimensions={0} | all-to-all | bytes 294912 | tf_op jit(solution)/shard_map/all_to_all | solution.py:37
  145.7 0.1 fusion.11
  146.3 0.7 fusion.8
  (70 shorter events, 1.7 us)
Async XLA Ops:
  30.4 5.9 %copy-start.1 = (s32[1536]{0:T(1024)S(1)}, s32[1536]{0:T(1024)}, u32[]{:S(2)}) copy-start(s32[1536]{0:T(1024)} %param.7) | copy-start | bytes 18436
  31.8 20.7 %all-to-all-start.2 = ((bf16[4,32,6,1024]{3,1,2,0:T(8,128)(2,1)}), bf16[4,32,6,1024]{3,1,2,0:T(8,128)(2,1)}, u32[]{:S(2)}, u32[]{:S(2)}) async-start(bf16[4,32,6,1024]{3,1,2,0:T(8,128)(2,1)} %stack.14), calls=%async_computation.2 | async-start | bytes 3145728 | tf_op jit(solution)/shard_map/all_to_all | solution.py:23
  69.0 3.3 %copy-start = (bf16[8,4,4,2,6,1024]{5,4,3,2,1,0:T(8,128)(2,1)S(1)}, bf16[8,4,4,2,6,1024]{5,4,3,2,1,0:T(8,128)(2,1)}, u32[]{:S(2)}) copy-start(bf16[8,4,4,2,6,1024]{5,4,3,2,1,0:T(8,128)(2,1)} %gather.7) | copy-start | bytes 9437188
